TPU v7x, 768 devices: a whole 4x8x12 slice. The times are simulated.
768 devices in a mesh: lat: 12 (over z), lon: 64 (over y, x, core).
Axes of the slice: x: 4, y: 8, z: 12, core: 2. Of those that a mesh axis runs over, the one named last changes fastest.
Arguments:
- fields: float32 [96, 2880, 384], P('lat', 'lon'), may hold values from -6 to 6
- cutoff: int32 [96], P('lat'), may hold values from 1 to 1425, as said below
Outputs:
- filtered: float32 [96, 2880, 384], P('lat', 'lon')
Inputs may be any that keep to these rules, and one draw needn't show every extreme that they name: cutoff[g] lies between 1 and 1 + (1439)(2 p + 1) // 96, where p is the number of rows between row g and the nearer pole; this ceiling grows from the pole rows to the equator.
All inputs are finite; a program needn't handle non-finite values.
Results may differ from a plain program's by a relative error of at most 0.0003.
Values sent between devices are 32-bit elements; how exact they have to be, the bound alone decides.
A program may use at most 64 MiB of HBM per device.

v0:
```python
import functools
import math

import jax
import jax.numpy as jnp
from jax import lax
from jax.experimental import pallas as pl
from jax.experimental.pallas import tpu as pltpu
from jax.sharding import PartitionSpec as P

MESH = pl.DeviceIdType.MESH
F32 = jnp.float32
BF16 = jnp.bfloat16
NLON = 2880
SEG = 45
PAD = 48
HALF = 23
SLOT = 24
ROWS = 8
LANES = 128
BLOCKS = 3
CHUNKS = 6
ORDER = (4, 3, 5, 2, 6, 1, 7)
HUB = 4
X_LAG = 2
R_LAG = 4
HALF_ROOT = math.sqrt(0.5)


FIRST_WAVES = (0, 8, 16, 24, 4, 20, 36, 52, 32)
COS_TERMS = [(-1) ** i / math.factorial(2 * i) for i in range(11)]
SIN_TERMS = [(-1) ** i / math.factorial(2 * i + 1) for i in range(11)]


def cos_sin(angle):
    square = angle * angle
    cos, sin = COS_TERMS[-1], SIN_TERMS[-1]
    for i in reversed(range(10)):
        cos, sin = cos * square + COS_TERMS[i], sin * square + SIN_TERMS[i]
    return cos, sin * angle


def wave_at(step):
    step = step - NLON * jnp.floor(step * (1.0 / NLON) + 0.5)
    return cos_sin(step * (2.0 * math.pi / NLON))


def real_dft(v):
    s = [v[i] + v[i + 4] for i in range(4)]
    d = [v[i] - v[i + 4] for i in range(4)]
    even, odd = s[0] + s[2], s[1] + s[3]
    minus = (d[1] - d[3]) * HALF_ROOT
    plus = (d[1] + d[3]) * HALF_ROOT
    return [
        (even + odd, even - odd),
        (d[0] + minus, -d[2] - plus),
        (s[0] - s[2], s[3] - s[1]),
        (d[0] - minus, d[2] - plus),
    ]


def real_idft(pairs):
    (a0, a4), (b_re, b_im), (c_re, c_im), (d_re, d_im) = pairs
    plus, minus = a0 + a4, a0 - a4
    c_re, c_im = c_re + c_re, c_im + c_im
    e = [plus + c_re, minus - c_im, plus - c_re, minus + c_im]
    diff = (b_re - d_re) * math.sqrt(2.0)
    both = (b_im + d_im) * math.sqrt(2.0)
    o = [2.0 * (b_re + d_re), diff - both, 2.0 * (d_im - b_im), -diff - both]
    return [e[i] + o[i] for i in range(4)] + [e[i] - o[i] for i in range(4)]


def turn_by(value, cos, sin):
    re, im = value
    return re * cos + im * sin, im * cos - re * sin


def add(a, b):
    return a[0] + b[0], a[1] + b[1]


def sub(a, b):
    return a[0] - b[0], a[1] - b[1]


def dft4(v):
    s02, d02, s13, d13 = add(v[0], v[2]), sub(v[0], v[2]), add(v[1], v[3]), sub(v[1], v[3])
    return [
        add(s02, s13),
        (d02[0] + d13[1], d02[1] - d13[0]),
        sub(s02, s13),
        (d02[0] - d13[1], d02[1] + d13[0]),
    ]


def idft4(v):
    s02, d02, s13, d13 = add(v[0], v[2]), sub(v[0], v[2]), add(v[1], v[3]), sub(v[1], v[3])
    return [
        add(s02, s13),
        (d02[0] - d13[1], d02[1] + d13[0]),
        sub(s02, s13),
        (d02[0] + d13[1], d02[1] - d13[0]),
    ]


def dft8(v):
    even = dft4([add(v[i], v[i + 4]) for i in range(4)])
    odd = [sub(v[i], v[i + 4]) for i in range(4)]
    odd = [
        odd[0],
        ((odd[1][0] + odd[1][1]) * HALF_ROOT, (odd[1][1] - odd[1][0]) * HALF_ROOT),
        (odd[2][1], -odd[2][0]),
        ((odd[3][1] - odd[3][0]) * HALF_ROOT, -(odd[3][0] + odd[3][1]) * HALF_ROOT),
    ]
    odd = dft4(odd)
    return [part[i] for i in range(4) for part in (even, odd)]


def idft8(v):
    even = idft4(v[0::2])
    odd = idft4(v[1::2])
    odd = [
        odd[0],
        ((odd[1][0] - odd[1][1]) * HALF_ROOT, (odd[1][1] + odd[1][0]) * HALF_ROOT),
        (-odd[2][1], odd[2][0]),
        (-(odd[3][0] + odd[3][1]) * HALF_ROOT, (odd[3][0] - odd[3][1]) * HALF_ROOT),
    ]
    return [add(even[i], odd[i]) for i in range(4)] + [sub(even[i], odd[i]) for i in range(4)]


SIXTEENTH = [(math.cos(math.pi * i / 8), math.sin(math.pi * i / 8)) for i in range(4)]


def first_chip_dft(z):
    low = real_dft([v[0] for v in z])
    turned = [turn_by((z[i][1], -z[i + 4][1]), *SIXTEENTH[i]) for i in range(4)]
    return low + dft4(turned)


def first_chip_idft(pairs):
    low = real_idft(pairs[:4])
    turned = idft4(pairs[4:])
    turned = [turn_by(turned[i], SIXTEENTH[i][0], -SIXTEENTH[i][1]) for i in range(4)]
    high = [2.0 * t[0] for t in turned] + [-2.0 * t[1] for t in turned]
    return list(zip(low, high))


def other_chip_dft(z, twist):
    return dft8([z[0]] + [turn_by(z[j], *twist[j]) for j in range(1, 8)])


def other_chip_idft(pairs, twist):
    z = idft8(pairs)
    return [z[0]] + [turn_by(z[j], twist[j][0], -twist[j][1]) for j in range(1, 8)]


def kernel(
    bands,
    cut_hbm,
    x_hbm,
    out,
    cut_ref,
    twist_ref,
    y_send,
    y_in,
    x_send,
    x_in,
    r_send,
    r_in,
    o_send,
    o_in,
    gate,
    stage,
    result,
    load_sem,
    ys_sem,
    yr_sem,
    xs_sem,
    xr_sem,
    rs_sem,
    rr_sem,
    os_sem,
    or_sem,
    meet_sem,
    go_sem,
):
    band = lax.axis_index("lat")
    lon = lax.axis_index("lon")
    y, j = lon // 8, lon % 8
    x, core = j // 2, j % 2
    total_rows = bands * ROWS

    def polar(row):
        return jnp.abs(2 * (band * ROWS + row) + 1 - total_rows) * 5 > 2 * total_rows

    count = sum(polar(row).astype(jnp.int32) for row in range(ROWS))
    first = jnp.where(polar(0), 0, ROWS - count)
    any_polar = count > 0

    def place(there):
        index = (there * count + 7) // 8
        return index, (index < count) & (index * 8 // jnp.maximum(count, 1) == there)

    index, mine = place(y)
    mine = mine & any_polar
    row_here = jnp.minimum(first + index, ROWS - 1)

    def keeper(c):
        return c % 2

    load = pltpu.make_async_copy(x_hbm, out, load_sem.at[0])
    cut_load = pltpu.make_async_copy(cut_hbm, cut_ref, load_sem.at[1])
    load.start()

    barrier = pltpu.get_barrier_semaphore()

    @pl.when(any_polar)
    def _():
        for step in ORDER:
            pl.semaphore_signal(barrier, inc=1, device_id=(band, (y + step) % 8 * 8 + j), device_id_type=MESH)

        @pl.when(y == HUB)
        def _():
            for step in range(1, 8):
                pl.semaphore_signal(barrier, inc=1, device_id=(band, y * 8 + (j + step) % 8), device_id_type=MESH)

    cut_load.start()
    load.wait()

    def y_copy(c, there, row, sender):
        return pltpu.make_async_remote_copy(
            src_ref=y_send.at[c, row, pl.ds(0, HALF)],
            dst_ref=y_in.at[c, sender, pl.ds(0, HALF)],
            send_sem=ys_sem,
            recv_sem=yr_sem.at[c],
            device_id=(band, there * 8 + j),
            device_id_type=MESH,
        )

    def x_copy(c, group, sender):
        return pltpu.make_async_remote_copy(
            src_ref=x_send.at[c, group, :, pl.ds(0, HALF)],
            dst_ref=x_in.at[c, sender, :, pl.ds(0, HALF)],
            send_sem=xs_sem.at[(core == keeper(c)).astype(jnp.int32)],
            recv_sem=xr_sem.at[c],
            device_id=(band, y * 8 + group * 2 + keeper(c)),
            device_id_type=MESH,
        )

    def r_copy(c, there, sender):
        return pltpu.make_async_remote_copy(
            src_ref=r_send.at[c, there, :, pl.ds(0, HALF)],
            dst_ref=r_in.at[c, sender, :, pl.ds(0, HALF)],
            send_sem=rs_sem,
            recv_sem=rr_sem.at[c],
            device_id=(band, y * 8 + there),
            device_id_type=MESH,
        )

    def o_copy(c, there, row, sender):
        return pltpu.make_async_remote_copy(
            src_ref=o_send.at[c, there, pl.ds(0, HALF)],
            dst_ref=o_in.at[c, row, pl.ds(0, HALF)],
            send_sem=os_sem,
            recv_sem=or_sem.at[c],
            device_id=(band, there * 8 + j),
            device_id_type=MESH,
        )

    def await_bytes(ref, sem):
        pltpu.make_async_copy(ref, ref, sem).wait()

    def await_parts(ref_of, sem, parts, choices):
        for choice in choices:

            @pl.when(parts == choice)
            def _():
                await_bytes(ref_of(choice), sem)

    rows_used = pl.ds(0, HALF)
    others = count - mine.astype(jnp.int32)

    low_lanes = lax.broadcasted_iota(jnp.int32, (HALF, LANES), 1) < 64

    def swap(value):
        return pltpu.roll(value, 64, 1)

    @pl.when(any_polar)
    def _():
        @pl.loop(0, ROWS)
        def _(row):
            for b in range(BLOCKS):
                upper = out[pl.ds(b * ROWS + row, HALF, stride=BLOCKS * ROWS), :]
                lower = out[pl.ds((HALF - 1) * BLOCKS * ROWS + b * ROWS + row, HALF, stride=BLOCKS * ROWS), :]
                y_send[2 * b, row, pl.ds(0, HALF), :] = jnp.where(low_lanes, upper, swap(lower))
                y_send[2 * b + 1, row, pl.ds(0, HALF), :] = jnp.where(low_lanes, swap(upper), lower)

        @pl.when(y == HUB)
        def _():
            pl.semaphore_wait(barrier, 14)
            for step in range(1, 8):
                pl.semaphore_signal(meet_sem, inc=1, device_id=(band, y * 8 + (j + step) % 8), device_id_type=MESH)

        @pl.when(y != HUB)
        def _():
            pl.semaphore_wait(barrier, 7)

        @pl.loop(0, CHUNKS)
        def _(c):
            for step in ORDER:
                there = (y + step) % 8
                index_there, holds = place(there)

                @pl.when(holds)
                def _():
                    y_copy(c, there, first + index_there, y).start()

        @pl.when(y == HUB)
        def _():
            pl.semaphore_wait(meet_sem, 7)
            for step in ORDER:
                pl.semaphore_signal(go_sem, inc=1, device_id=(band, (y + step) % 8 * 8 + j), device_id_type=MESH)

    cut_load.wait()

    def build_gates():
        shape = (PAD, LANES)
        down = lax.broadcasted_iota(jnp.int32, shape, 0)
        across = lax.broadcasted_iota(jnp.int32, shape, 1)

        def longitude(slot):
            return jnp.where(slot < SLOT, slot, slot - SLOT + HALF - 1).astype(F32)

        slot = jnp.where(across < 64, across, jnp.where(across < 64 + SLOT, across - 64 + SLOT, across - 64 - SLOT))
        valid = (slot != HALF) & (slot != SLOT) & (slot < PAD - 1) & (slot >= 0)
        valid = valid & (down < SEG) & ((across < PAD) | ((across >= 64) & (across < 64 + PAD)))
        m_across, m_down = longitude(slot), longitude(down)
        valid_left = (down != HALF) & (down != PAD - 1) & (across < SEG)
        k_down, k_across = 64.0 * down.astype(F32), 64.0 * across.astype(F32)
        upper_rows, used = down < SLOT, across < PAD
        cut = jnp.full(shape, cut_ref[row_here].astype(F32), F32)
        top = cos_sin(cut * (math.pi / NLON))[1]
        rows = lax.broadcasted_iota(jnp.int32, (8, LANES), 0)
        twist_ref[0:8], twist_ref[8:16] = wave_at((rows * x * SEG).astype(F32))

        def ordered(block):
            return jnp.where(used, jnp.where(upper_rows, block, swap(block)), 0.0)

        def circulant(p, base):
            wave = base + k_down
            cos_right, sin_right = wave_at(wave * m_across)
            folded = jnp.minimum(wave, NLON - wave)
            ratio = top / cos_sin(jnp.maximum(folded, 1.0) * (math.pi / NLON))[1]
            gain = jnp.where(valid, jnp.where(folded <= cut, 1.0, ratio * ratio) * (1.0 / NLON), 0.0)
            cos_right, sin_right = gain * cos_right, gain * sin_right
            cos_left, sin_left = wave_at((base + k_across) * m_down)
            cos_left = jnp.where(valid_left, cos_left, 0.0)[:, :PAD]
            sin_left = jnp.where(valid_left, sin_left, 0.0)[:, :PAD]
            dot = functools.partial(jnp.dot, precision=lax.Precision.HIGHEST, preferred_element_type=F32)
            real = dot(cos_left, cos_right) + dot(sin_left, sin_right)
            imag = dot(sin_left, cos_right) - dot(cos_left, sin_right)
            return ordered(real), ordered(imag)

        def put(p, real, lower, imag):
            block = jnp.concatenate(
                [real - pltpu.roll(imag, PAD, 1), imag + pltpu.roll(lower, PAD, 1)], axis=0
            )
            top_part = block.astype(BF16)
            gate[p, 0 : 2 * PAD] = top_part
            gate[p, 2 * PAD : 4 * PAD] = (block - top_part.astype(F32)).astype(BF16)

        @pl.loop(0, 8)
        def _(p):
            base = x + 8 * p
            for i in range(8):
                base = jnp.where((x == 0) & (p == i), FIRST_WAVES[i], base)
            real, imag = circulant(p, base.astype(F32))
            put(p, real, real, imag)

        @pl.when(x == 0)
        def _():
            put(0, circulant(0, 0.0)[0], circulant(0, float(FIRST_WAVES[8]))[0], jnp.zeros(shape, F32))

    def y_stage(c):
        await_bytes(y_in.at[c, pl.ds(0, 7), rows_used], yr_sem.at[c])
        y_in[c, y, pl.ds(0, HALF)] = y_send[c, row_here, pl.ds(0, HALF)]
        @pl.loop(0, SLOT, step=8)
        def _(m):
            rows = pl.ds(pl.multiple_of(m, 8), 8)
            pairs = real_dft([y_in[c, i, rows] for i in range(8)])
            for group in range(4):
                x_send[c, group, 0, rows], x_send[c, group, 1, rows] = pairs[group]

        @pl.when((c == 0) & (y != HUB))
        def _():
            pl.semaphore_wait(go_sem, 1)

        for group in range(4):
            self_held = (x == group) & (core == keeper(c))

            @pl.when(self_held)
            def _():
                x_in[c, j, :, pl.ds(0, HALF)] = x_send[c, group, :, pl.ds(0, HALF)]

            @pl.when(jnp.logical_not(self_held))
            def _():
                x_copy(c, group, j).start()

    def x_stage(c):
        await_bytes(x_in.at[c, pl.ds(0, 7), :, rows_used], xr_sem.at[c])
        twist = [(twist_ref[i : i + 1], twist_ref[8 + i : 9 + i]) for i in range(8)]
        eight = lax.broadcasted_iota(jnp.int32, (8, LANES), 0)
        low_eight = lax.broadcasted_iota(jnp.int32, (8, LANES), 1) < 64

        def take(i, part, m):
            return jnp.where(eight < HALF - m, x_in[c, i, part, pl.ds(m, 8)], 0.0)

        def write(pairs, m):
            for p in range(8):
                for part in range(2):
                    stage[p, pl.ds(part * PAD + m, 8)] = pairs[p][part]
                    stage[p, pl.ds(part * PAD + SLOT + m, 8)] = swap(pairs[p][part])

        @pl.when(x == 0)
        def _():
            @pl.loop(0, SLOT, step=8)
            def _(m):
                m = pl.multiple_of(m, 8)
                write(first_chip_dft([(take(i, 0, m), take(i, 1, m)) for i in range(8)]), m)

        @pl.when(x != 0)
        def _():
            @pl.loop(0, SLOT, step=8)
            def _(m):
                m = pl.multiple_of(m, 8)
                write(other_chip_dft([(take(i, 0, m), take(i, 1, m)) for i in range(8)], twist), m)

        for p in range(8):
            value = stage[p]
            big = value.astype(BF16)
            small_part = (value - big.astype(F32)).astype(BF16)
            both = jnp.dot(gate[p, :, 0 : 2 * PAD], big, preferred_element_type=F32)
            rest = jnp.dot(gate[p, 0 : 2 * PAD, 0 : 2 * PAD], small_part, preferred_element_type=F32)
            result[p] = both[0 : 2 * PAD] + both[2 * PAD : 4 * PAD] + rest

        def pairs_at(m):
            def pick(p, part):
                return jnp.where(
                    low_eight, result[p, pl.ds(part * PAD + m, 8)], result[p, pl.ds(part * PAD + SLOT + m, 8)]
                )

            return [(pick(p, 0), pick(p, 1)) for p in range(8)]

        def write_back(z, m):
            for i in range(8):
                r_send[c, i, 0, pl.ds(m, 8)], r_send[c, i, 1, pl.ds(m, 8)] = z[i]

        @pl.when(x == 0)
        def _():
            @pl.loop(0, SLOT, step=8)
            def _(m):
                m = pl.multiple_of(m, 8)
                write_back(first_chip_idft(pairs_at(m)), m)

        @pl.when(x != 0)
        def _():
            @pl.loop(0, SLOT, step=8)
            def _(m):
                m = pl.multiple_of(m, 8)
                write_back(other_chip_idft(pairs_at(m), twist), m)

        for step in (4, 5, 3, 2, 6, 7, 1):
            r_copy(c, (j + step) % 8, x).start()
        r_in[c, x, :, pl.ds(0, HALF)] = r_send[c, j, :, pl.ds(0, HALF)]

    def r_stage(c):
        await_parts(
            lambda n: r_in.at[c, pl.ds(0, n), :, rows_used],
            rr_sem.at[c],
            4 - (core == keeper(c)).astype(jnp.int32),
            (3, 4),
        )

        @pl.loop(0, SLOT, step=8)
        def _(m):
            rows = pl.ds(pl.multiple_of(m, 8), 8)
            values = real_idft([(r_in[c, g, 0, rows], r_in[c, g, 1, rows]) for g in range(4)])
            for i in range(8):
                o_send[c, i, rows] = values[i]
        for step in ORDER:
            o_copy(c, (y + step) % 8, row_here, y).start()
        o_in[c, row_here, pl.ds(0, HALF)] = o_send[c, y, pl.ds(0, HALF)]

    @pl.when(mine)
    def _():
        build_gates()

        @pl.loop(0, CHUNKS + R_LAG)
        def _(t):
            @pl.when(t < CHUNKS)
            def _():
                y_stage(t)

            @pl.when((t >= X_LAG) & (t < CHUNKS + X_LAG) & (core == keeper(t - X_LAG)))
            def _():
                x_stage(t - X_LAG)

            @pl.when(t >= R_LAG)
            def _():
                r_stage(t - R_LAG)

    @pl.when(any_polar & jnp.logical_not(mine) & (y != HUB))
    def _():
        pl.semaphore_wait(go_sem, 1)

    @pl.when(any_polar)
    def _():
        @pl.loop(0, BLOCKS)
        def _(b):
            for c in (2 * b, 2 * b + 1):
                await_parts(lambda n: o_in.at[c, pl.ds(0, n), rows_used], or_sem.at[c], others, range(1, 8))

            @pl.loop(0, ROWS)
            def _(row):
                @pl.when(polar(row))
                def _():
                    left, right = o_in[2 * b, row, pl.ds(0, HALF), :], o_in[2 * b + 1, row, pl.ds(0, HALF), :]
                    start = b * ROWS + row
                    out[pl.ds(start, HALF, stride=BLOCKS * ROWS), :] = jnp.where(low_lanes, left, swap(right))
                    out[pl.ds((HALF - 1) * BLOCKS * ROWS + start, HALF, stride=BLOCKS * ROWS), :] = jnp.where(
                        low_lanes, swap(left), right
                    )

        await_parts(lambda n: y_send.at[:, pl.ds(0, n), rows_used], ys_sem, others, range(1, 8))

    @pl.when(mine)
    def _():
        await_bytes(x_send.at[pl.ds(0, CHUNKS // 2), :, :, rows_used], xs_sem.at[0])
        await_bytes(x_send.at[pl.ds(0, CHUNKS // 2), pl.ds(0, 3), :, rows_used], xs_sem.at[1])
        await_bytes(r_send.at[pl.ds(0, CHUNKS // 2), pl.ds(0, 7), :, rows_used], rs_sem)
        await_bytes(o_send.at[:, pl.ds(0, 7), rows_used], os_sem)


def local(bands, fields, cutoff):
    flat = jnp.transpose(fields.reshape(ROWS, SEG, BLOCKS, LANES), (1, 2, 0, 3)).reshape(SEG * BLOCKS * ROWS, LANES)
    vmem, dma = pltpu.VMEM, pltpu.SemaphoreType.DMA
    hbm = pl.BlockSpec(memory_space=pltpu.HBM)
    out = pl.pallas_call(
        functools.partial(kernel, bands),
        out_shape=jax.ShapeDtypeStruct(flat.shape, F32),
        in_specs=[hbm] * 2,
        out_specs=pl.BlockSpec(memory_space=pltpu.VMEM),
        scratch_shapes=[
            pltpu.SMEM((ROWS,), jnp.int32),
            vmem((16, LANES), F32),
            vmem((CHUNKS, 8, SLOT, LANES), F32),
            vmem((CHUNKS, 8, SLOT, LANES), F32),
            vmem((CHUNKS, 4, 2, SLOT, LANES), F32),
            vmem((CHUNKS, 8, 2, SLOT, LANES), F32),
            vmem((CHUNKS, 8, 2, SLOT, LANES), F32),
            vmem((CHUNKS, 4, 2, SLOT, LANES), F32),
            vmem((CHUNKS, 8, SLOT, LANES), F32),
            vmem((CHUNKS, 8, SLOT, LANES), F32),
            vmem((8, 4 * PAD, LANES), BF16),
            vmem((8, 2 * PAD, LANES), F32),
            vmem((8, 2 * PAD, LANES), F32),
            dma((2,)),
            dma,
            dma((CHUNKS,)),
            dma((2,)),
            dma((CHUNKS,)),
            dma,
            dma((CHUNKS,)),
            dma,
            dma((CHUNKS,)),
            pltpu.SemaphoreType.REGULAR,
            pltpu.SemaphoreType.REGULAR,
        ],
        compiler_params=pltpu.CompilerParams(
            collective_id=0, has_side_effects=True, vmem_limit_bytes=54304 * 1024
        ),
    )(cutoff, flat)
    filtered = jnp.transpose(out.reshape(SEG, BLOCKS, ROWS, LANES), (2, 0, 1, 3))
    return filtered.reshape(ROWS, SEG, BLOCKS * LANES)


def solution(mesh):
    return jax.shard_map(
        functools.partial(local, mesh.shape["lat"]),
        mesh=mesh,
        in_specs=(P("lat", "lon", None), P("lat")),
        out_specs=P("lat", "lon", None),
        check_vma=False,
    )
```

profile of v0, /device:TPU:1, one launch (start us, length us, event | category | flops | bytes accessed | tf_op | source)
XLA Modules:
  0.0 45.5 jit_solution(2864567701395065594)
XLA Ops:
  0.0 0.0 copy-start
  0.0 0.7 %copy-done = s32[8]{0:T(128)S(1)} copy-done((s32[8]{0:T(128)S(1)}, s32[8]{0:T(128)}, u32[]{:S(2)}) %copy-start) | copy-done | bytes 56
  0.7 44.1 %shard_map.28 = f32[1080,128]{1,0:T(8,128)S(1)} custom-call(s32[8]{0:T(128)S(1)} %copy-done, f32[1080,128]{1,0:T(8,128)} %bitcast.11), custom_call_target="tpu_custom_call" | custom-call | tf_op jit(solution)/shard_map/pallas_call | solution.py:548
  44.7 0.8 %copy.4 = f32[8,45,384]{2,0,1:T(8,128)} copy(f32[8,45,384]{2,0,1:T(8,128)S(1)} %bitcast.10) | data formatting | bytes 1105920
Async XLA Ops:
  0.0 0.7 %copy-start = (s32[8]{0:T(128)S(1)}, s32[8]{0:T(128)}, u32[]{:S(2)}) copy-start(s32[8]{0:T(128)} %cut_hbm.1) | copy-start | bytes 100
where the time goes:
time: 45.7 us; the launch traced here: 45.5 us
  Pallas kernels  44.1 us (96%)
  local copies, waits for them, and re-layouts  1.46 us (3%)
    pallas_call x1, Pallas kernels, local(): pl.pallas_call(functools.partial(kernel, bands), out_shape=jax.ShapeDtype...  44.1 us
    unnamed x3, local copies, waits for them, and re-layouts  1.46 us

commit v1 on v0

--- a/solution.py
+++ b/solution.py
@@ -21,9 +21,7 @@
 BLOCKS = 3
 CHUNKS = 6
 ORDER = (4, 3, 5, 2, 6, 1, 7)
-HUB = 4
-X_LAG = 2
-R_LAG = 4
+HUB = 1
 HALF_ROOT = math.sqrt(0.5)
 
 
@@ -183,6 +181,7 @@
     or_sem,
     meet_sem,
     go_sem,
+    here_sem,
 ):
     band = lax.axis_index("lat")
     lon = lax.axis_index("lon")
@@ -212,17 +211,44 @@
     cut_load = pltpu.make_async_copy(cut_hbm, cut_ref, load_sem.at[1])
     load.start()
 
+    late_plane = band == 0
+    late = late_plane & (lon == 0)
+    late_column = late_plane & (j == 0) & (y != 0)
+    late_row = late_plane & (y == 0) & (j != 0)
+    x_lag = 2
+    r_lag = 4
+
     barrier = pltpu.get_barrier_semaphore()
 
-    @pl.when(any_polar)
+    def column_device(there):
+        return (band, there * 8 + j)
+
+    def row_device(there):
+        return (band, y * 8 + there)
+
+    def signal(sem, device):
+        pl.semaphore_signal(sem, inc=1, device_id=device, device_id_type=MESH)
+
+    @pl.when(any_polar & jnp.logical_not(late))
     def _():
         for step in ORDER:
-            pl.semaphore_signal(barrier, inc=1, device_id=(band, (y + step) % 8 * 8 + j), device_id_type=MESH)
+            signal(barrier, column_device((y + step) % 8))
 
         @pl.when(y == HUB)
         def _():
             for step in range(1, 8):
-                pl.semaphore_signal(barrier, inc=1, device_id=(band, y * 8 + (j + step) % 8), device_id_type=MESH)
+                signal(barrier, row_device((j + step) % 8))
+
+        @pl.when(late_row)
+        def _():
+            signal(barrier, row_device(0))
+
+    @pl.when(any_polar & late)
+    def _():
+        pl.semaphore_wait(barrier, 14)
+        for step in ORDER:
+            signal(here_sem, column_device((y + step) % 8))
+            signal(here_sem, row_device((j + step) % 8))
 
     cut_load.start()
     load.wait()
@@ -287,39 +313,41 @@
 
     @pl.when(any_polar)
     def _():
-        @pl.loop(0, ROWS)
-        def _(row):
-            for b in range(BLOCKS):
-                upper = out[pl.ds(b * ROWS + row, HALF, stride=BLOCKS * ROWS), :]
-                lower = out[pl.ds((HALF - 1) * BLOCKS * ROWS + b * ROWS + row, HALF, stride=BLOCKS * ROWS), :]
+        def pack(b):
+            for row in range(ROWS):
+                start = b * ROWS + row
+                upper = out[pl.ds(start, HALF, stride=BLOCKS * ROWS), :]
+                lower = out[pl.ds((HALF - 1) * BLOCKS * ROWS + start, HALF, stride=BLOCKS * ROWS), :]
                 y_send[2 * b, row, pl.ds(0, HALF), :] = jnp.where(low_lanes, upper, swap(lower))
                 y_send[2 * b + 1, row, pl.ds(0, HALF), :] = jnp.where(low_lanes, swap(upper), lower)
 
+        pack(0)
+        fewer = late_column.astype(jnp.int32)
+
         @pl.when(y == HUB)
         def _():
-            pl.semaphore_wait(barrier, 14)
+            pl.semaphore_wait(barrier, 14 - fewer)
             for step in range(1, 8):
-                pl.semaphore_signal(meet_sem, inc=1, device_id=(band, y * 8 + (j + step) % 8), device_id_type=MESH)
-
-        @pl.when(y != HUB)
-        def _():
-            pl.semaphore_wait(barrier, 7)
-
-        @pl.loop(0, CHUNKS)
-        def _(c):
-            for step in ORDER:
-                there = (y + step) % 8
-                index_there, holds = place(there)
-
-                @pl.when(holds)
-                def _():
-                    y_copy(c, there, first + index_there, y).start()
-
-        @pl.when(y == HUB)
-        def _():
-            pl.semaphore_wait(meet_sem, 7)
-            for step in ORDER:
-                pl.semaphore_signal(go_sem, inc=1, device_id=(band, (y + step) % 8 * 8 + j), device_id_type=MESH)
+                signal(meet_sem, row_device((j + step) % 8))
+
+        @pl.when((y != HUB) & jnp.logical_not(late))
+        def _():
+            pl.semaphore_wait(barrier, 7 - fewer)
+
+        @pl.loop(0, BLOCKS)
+        def _(b):
+            for c in (2 * b, 2 * b + 1):
+                for step in ORDER:
+                    there = (y + step) % 8
+                    index_there, holds = place(there)
+
+                    @pl.when(holds & jnp.logical_not(late_column & (there == 0)))
+                    def _():
+                        y_copy(c, there, first + index_there, y).start()
+
+            @pl.when(b < BLOCKS - 1)
+            def _():
+                pack(b + 1)
 
     cut_load.wait()
 
@@ -335,8 +363,9 @@
         valid = (slot != HALF) & (slot != SLOT) & (slot < PAD - 1) & (slot >= 0)
         valid = valid & (down < SEG) & ((across < PAD) | ((across >= 64) & (across < 64 + PAD)))
         m_across, m_down = longitude(slot), longitude(down)
-        valid_left = (down != HALF) & (down != PAD - 1) & (across < SEG)
-        k_down, k_across = 64.0 * down.astype(F32), 64.0 * across.astype(F32)
+        valid_left = (down != HALF) & (down != PAD - 1) & (across < 2 * PAD)
+        k_down = 64.0 * down.astype(F32)
+        k_across = 64.0 * jnp.where(across < PAD, across, across - PAD).astype(F32)
         upper_rows, used = down < SLOT, across < PAD
         cut = jnp.full(shape, cut_ref[row_here].astype(F32), F32)
         top = cos_sin(cut * (math.pi / NLON))[1]
@@ -346,40 +375,41 @@
         def ordered(block):
             return jnp.where(used, jnp.where(upper_rows, block, swap(block)), 0.0)
 
-        def circulant(p, base):
+        def circulant(base):
             wave = base + k_down
             cos_right, sin_right = wave_at(wave * m_across)
             folded = jnp.minimum(wave, NLON - wave)
             ratio = top / cos_sin(jnp.maximum(folded, 1.0) * (math.pi / NLON))[1]
             gain = jnp.where(valid, jnp.where(folded <= cut, 1.0, ratio * ratio) * (1.0 / NLON), 0.0)
-            cos_right, sin_right = gain * cos_right, gain * sin_right
+            right = jnp.concatenate([gain * cos_right, gain * sin_right], axis=0)
             cos_left, sin_left = wave_at((base + k_across) * m_down)
-            cos_left = jnp.where(valid_left, cos_left, 0.0)[:, :PAD]
-            sin_left = jnp.where(valid_left, sin_left, 0.0)[:, :PAD]
-            dot = functools.partial(jnp.dot, precision=lax.Precision.HIGHEST, preferred_element_type=F32)
-            real = dot(cos_left, cos_right) + dot(sin_left, sin_right)
-            imag = dot(sin_left, cos_right) - dot(cos_left, sin_right)
-            return ordered(real), ordered(imag)
-
-        def put(p, real, lower, imag):
-            block = jnp.concatenate(
-                [real - pltpu.roll(imag, PAD, 1), imag + pltpu.roll(lower, PAD, 1)], axis=0
-            )
+            left = jnp.concatenate([jnp.where(used, cos_left, sin_left), jnp.where(used, sin_left, -cos_left)], axis=0)
+            left = jnp.where(jnp.concatenate([valid_left] * 2, axis=0), left, 0.0)[:, : 2 * PAD]
+            left_high, right_high = left.astype(BF16), right.astype(BF16)
+            left_low = (left - left_high.astype(F32)).astype(BF16)
+            right_low = (right - right_high.astype(F32)).astype(BF16)
+            dot = functools.partial(jnp.dot, preferred_element_type=F32)
+            both = dot(left_high, right_high) + (dot(left_high, right_low) + dot(left_low, right_high))
+            return ordered(both[:PAD]), ordered(both[PAD:])
+
+        def put(p, start, block):
+            rows = block.shape[0]
             top_part = block.astype(BF16)
-            gate[p, 0 : 2 * PAD] = top_part
-            gate[p, 2 * PAD : 4 * PAD] = (block - top_part.astype(F32)).astype(BF16)
-
-        @pl.loop(0, 8)
+            gate[p, pl.ds(start, rows)] = top_part
+            gate[p, pl.ds(start + 2 * PAD, rows)] = (block - top_part.astype(F32)).astype(BF16)
+
+        @pl.loop(0, 8, unroll=2)
         def _(p):
             base = x + 8 * p
             for i in range(8):
                 base = jnp.where((x == 0) & (p == i), FIRST_WAVES[i], base)
-            real, imag = circulant(p, base.astype(F32))
-            put(p, real, real, imag)
+            real, imag = circulant(base.astype(F32))
+            put(p, 0, real - pltpu.roll(imag, PAD, 1))
+            put(p, PAD, imag + pltpu.roll(real, PAD, 1))
 
         @pl.when(x == 0)
         def _():
-            put(0, circulant(0, 0.0)[0], circulant(0, float(FIRST_WAVES[8]))[0], jnp.zeros(shape, F32))
+            put(0, PAD, pltpu.roll(circulant(float(FIRST_WAVES[8]))[0], PAD, 1))
 
     def y_stage(c):
         await_bytes(y_in.at[c, pl.ds(0, 7), rows_used], yr_sem.at[c])
@@ -391,12 +421,17 @@
             for group in range(4):
                 x_send[c, group, 0, rows], x_send[c, group, 1, rows] = pairs[group]
 
-        @pl.when((c == 0) & (y != HUB))
+        @pl.when((c == 0) & (y != HUB) & jnp.logical_not(late))
         def _():
             pl.semaphore_wait(go_sem, 1)
 
-        for group in range(4):
+        for group in (3, 2, 1, 0):
             self_held = (x == group) & (core == keeper(c))
+            if group == 0:
+
+                @pl.when((c == 0) & late_row)
+                def _():
+                    pl.semaphore_wait(here_sem, 1)
 
             @pl.when(self_held)
             def _():
@@ -495,23 +530,49 @@
     def _():
         build_gates()
 
-        @pl.loop(0, CHUNKS + R_LAG)
+    @pl.when(any_polar & (y == HUB))
+    def _():
+        pl.semaphore_wait(meet_sem, 7)
+        for step in ORDER:
+            there = (y + step) % 8
+
+            @pl.when(jnp.logical_not(late_column & (there == 0)))
+            def _():
+                signal(go_sem, column_device(there))
+
+    @pl.when(any_polar & late_column)
+    def _():
+        pl.semaphore_wait(here_sem, 1)
+
+        @pl.when(place(0)[1])
+        def _():
+            @pl.loop(0, CHUNKS)
+            def _(c):
+                y_copy(c, 0, first, y).start()
+
+    @pl.when(mine)
+    def _():
+        @pl.loop(0, CHUNKS + r_lag)
         def _(t):
             @pl.when(t < CHUNKS)
             def _():
                 y_stage(t)
 
-            @pl.when((t >= X_LAG) & (t < CHUNKS + X_LAG) & (core == keeper(t - X_LAG)))
-            def _():
-                x_stage(t - X_LAG)
-
-            @pl.when(t >= R_LAG)
-            def _():
-                r_stage(t - R_LAG)
-
-    @pl.when(any_polar & jnp.logical_not(mine) & (y != HUB))
+            @pl.when((t >= x_lag) & (t < CHUNKS + x_lag) & (core == keeper(t - x_lag)))
+            def _():
+                x_stage(t - x_lag)
+
+            @pl.when(t >= r_lag)
+            def _():
+                r_stage(t - r_lag)
+
+    @pl.when(any_polar & jnp.logical_not(mine | late) & (y != HUB))
     def _():
         pl.semaphore_wait(go_sem, 1)
+
+        @pl.when(late_row)
+        def _():
+            pl.semaphore_wait(here_sem, 1)
 
     @pl.when(any_polar)
     def _():
@@ -520,16 +581,23 @@
             for c in (2 * b, 2 * b + 1):
                 await_parts(lambda n: o_in.at[c, pl.ds(0, n), rows_used], or_sem.at[c], others, range(1, 8))
 
-            @pl.loop(0, ROWS)
-            def _(row):
-                @pl.when(polar(row))
-                def _():
-                    left, right = o_in[2 * b, row, pl.ds(0, HALF), :], o_in[2 * b + 1, row, pl.ds(0, HALF), :]
-                    start = b * ROWS + row
-                    out[pl.ds(start, HALF, stride=BLOCKS * ROWS), :] = jnp.where(low_lanes, left, swap(right))
-                    out[pl.ds((HALF - 1) * BLOCKS * ROWS + start, HALF, stride=BLOCKS * ROWS), :] = jnp.where(
-                        low_lanes, swap(left), right
-                    )
+            def unpack(row):
+                left, right = o_in[2 * b, row, pl.ds(0, HALF), :], o_in[2 * b + 1, row, pl.ds(0, HALF), :]
+                start = b * ROWS + row
+                out[pl.ds(start, HALF, stride=BLOCKS * ROWS), :] = jnp.where(low_lanes, left, swap(right))
+                out[pl.ds((HALF - 1) * BLOCKS * ROWS + start, HALF, stride=BLOCKS * ROWS), :] = jnp.where(
+                    low_lanes, swap(left), right
+                )
+
+            @pl.when(count == ROWS)
+            def _():
+                for row in range(ROWS):
+                    unpack(row)
+
+            @pl.when(count < ROWS)
+            def _():
+                for row in range(ROWS):
+                    pl.when(polar(row))(functools.partial(unpack, row))
 
         await_parts(lambda n: y_send.at[:, pl.ds(0, n), rows_used], ys_sem, others, range(1, 8))
 
@@ -575,6 +643,7 @@
             dma((CHUNKS,)),
             pltpu.SemaphoreType.REGULAR,
             pltpu.SemaphoreType.REGULAR,
+            pltpu.SemaphoreType.REGULAR,
         ],
         compiler_params=pltpu.CompilerParams(
             collective_id=0, has_side_effects=True, vmem_limit_bytes=54304 * 1024

time: 45.7 us -> 44 us (0.963)
  Pallas kernels: 44.1 us -> 42.4 us
    pallas_call x1, Pallas kernels: 44.1 us -> 42.4 us  [local(): pl.pallas_call(functools.partial(kernel, bands), out_shape=jax.ShapeDtype...]
where the time goes in v1:
time: 44 us; the launch traced here: 43.8 us
  Pallas kernels  42.4 us (96%)
  local copies, waits for them, and re-layouts  1.46 us (3%)
    pallas_call x1, Pallas kernels, local(): pl.pallas_call(functools.partial(kernel, bands), out_shape=jax.ShapeDtype...  42.4 us
    unnamed x3, local copies, waits for them, and re-layouts  1.46 us

profile of v1, /device:TPU:1, one launch (start us, length us, event | category | flops | bytes accessed | tf_op | source)
XLA Modules:
  0.0 43.8 jit_solution(5360306793911318206)
XLA Ops:
  0.0 0.0 copy-start
  0.0 0.7 %copy-done = s32[8]{0:T(128)S(1)} copy-done((s32[8]{0:T(128)S(1)}, s32[8]{0:T(128)}, u32[]{:S(2)}) %copy-start) | copy-done | bytes 56
  0.7 42.4 %shard_map.28 = f32[1080,128]{1,0:T(8,128)S(1)} custom-call(s32[8]{0:T(128)S(1)} %copy-done, f32[1080,128]{1,0:T(8,128)} %bitcast.11), custom_call_target="tpu_custom_call" | custom-call | tf_op jit(solution)/shard_map/pallas_call | solution.py:616
  43.0 0.8 %copy.4 = f32[8,45,384]{2,0,1:T(8,128)} copy(f32[8,45,384]{2,0,1:T(8,128)S(1)} %bitcast.10) | data formatting | bytes 1105920
Async XLA Ops:
  0.0 0.7 %copy-start = (s32[8]{0:T(128)S(1)}, s32[8]{0:T(128)}, u32[]{:S(2)}) copy-start(s32[8]{0:T(128)} %cut_hbm.1) | copy-start | bytes 100

commit v2 on v1

--- a/solution.py
+++ b/solution.py
@@ -182,6 +182,9 @@
     meet_sem,
     go_sem,
     here_sem,
+    y_relay,
+    relay_sem,
+    pass_sem,
 ):
     band = lax.axis_index("lat")
     lon = lax.axis_index("lon")
@@ -215,6 +218,7 @@
     late = late_plane & (lon == 0)
     late_column = late_plane & (j == 0) & (y != 0)
     late_row = late_plane & (y == 0) & (j != 0)
+    relay = late_plane & (lon == 1)
     x_lag = 2
     r_lag = 4
 
@@ -242,6 +246,11 @@
         @pl.when(late_row)
         def _():
             signal(barrier, row_device(0))
+
+        @pl.when(relay)
+        def _():
+            for step in ORDER:
+                signal(barrier, (band, step * 8))
 
     @pl.when(any_polar & late)
     def _():
@@ -263,6 +272,26 @@
             device_id_type=MESH,
         )
 
+    def relay_copy(c):
+        return pltpu.make_async_remote_copy(
+            src_ref=y_send.at[c, first, pl.ds(0, HALF)],
+            dst_ref=y_relay.at[c, y, pl.ds(0, HALF)],
+            send_sem=ys_sem,
+            recv_sem=relay_sem.at[c],
+            device_id=(band, 1),
+            device_id_type=MESH,
+        )
+
+    def pass_copy(c):
+        return pltpu.make_async_remote_copy(
+            src_ref=y_relay.at[c, pl.ds(1, 7), pl.ds(0, HALF)],
+            dst_ref=y_in.at[c, pl.ds(1, 7), pl.ds(0, HALF)],
+            send_sem=pass_sem,
+            recv_sem=yr_sem.at[c],
+            device_id=(band, 0),
+            device_id_type=MESH,
+        )
+
     def x_copy(c, group, sender):
         return pltpu.make_async_remote_copy(
             src_ref=x_send.at[c, group, :, pl.ds(0, HALF)],
@@ -322,17 +351,15 @@
                 y_send[2 * b + 1, row, pl.ds(0, HALF), :] = jnp.where(low_lanes, swap(upper), lower)
 
         pack(0)
-        fewer = late_column.astype(jnp.int32)
-
         @pl.when(y == HUB)
         def _():
-            pl.semaphore_wait(barrier, 14 - fewer)
+            pl.semaphore_wait(barrier, 14)
             for step in range(1, 8):
                 signal(meet_sem, row_device((j + step) % 8))
 
         @pl.when((y != HUB) & jnp.logical_not(late))
         def _():
-            pl.semaphore_wait(barrier, 7 - fewer)
+            pl.semaphore_wait(barrier, 7)
 
         @pl.loop(0, BLOCKS)
         def _(b):
@@ -341,9 +368,15 @@
                     there = (y + step) % 8
                     index_there, holds = place(there)
 
-                    @pl.when(holds & jnp.logical_not(late_column & (there == 0)))
+                    by_relay = late_column & (there == 0)
+
+                    @pl.when(holds & jnp.logical_not(by_relay))
                     def _():
                         y_copy(c, there, first + index_there, y).start()
+
+                    @pl.when(holds & by_relay)
+                    def _():
+                        relay_copy(c).start()
 
             @pl.when(b < BLOCKS - 1)
             def _():
@@ -441,6 +474,11 @@
             def _():
                 x_copy(c, group, j).start()
 
+        @pl.when(relay)
+        def _():
+            await_bytes(y_relay.at[c, pl.ds(0, 7), rows_used], relay_sem.at[c])
+            pass_copy(c).start()
+
     def x_stage(c):
         await_bytes(x_in.at[c, pl.ds(0, 7), :, rows_used], xr_sem.at[c])
         twist = [(twist_ref[i : i + 1], twist_ref[8 + i : 9 + i]) for i in range(8)]
@@ -522,14 +560,14 @@
             values = real_idft([(r_in[c, g, 0, rows], r_in[c, g, 1, rows]) for g in range(4)])
             for i in range(8):
                 o_send[c, i, rows] = values[i]
+        @pl.when((c == 0) & late_column)
+        def _():
+            pl.semaphore_wait(here_sem, 1)
+
         for step in ORDER:
             o_copy(c, (y + step) % 8, row_here, y).start()
         o_in[c, row_here, pl.ds(0, HALF)] = o_send[c, y, pl.ds(0, HALF)]
 
-    @pl.when(mine)
-    def _():
-        build_gates()
-
     @pl.when(any_polar & (y == HUB))
     def _():
         pl.semaphore_wait(meet_sem, 7)
@@ -540,15 +578,9 @@
             def _():
                 signal(go_sem, column_device(there))
 
-    @pl.when(any_polar & late_column)
-    def _():
-        pl.semaphore_wait(here_sem, 1)
-
-        @pl.when(place(0)[1])
-        def _():
-            @pl.loop(0, CHUNKS)
-            def _(c):
-                y_copy(c, 0, first, y).start()
+    @pl.when(mine)
+    def _():
+        build_gates()
 
     @pl.when(mine)
     def _():
@@ -570,7 +602,7 @@
     def _():
         pl.semaphore_wait(go_sem, 1)
 
-        @pl.when(late_row)
+        @pl.when(late_row | late_column)
         def _():
             pl.semaphore_wait(here_sem, 1)
 
@@ -607,6 +639,10 @@
         await_bytes(x_send.at[pl.ds(0, CHUNKS // 2), pl.ds(0, 3), :, rows_used], xs_sem.at[1])
         await_bytes(r_send.at[pl.ds(0, CHUNKS // 2), pl.ds(0, 7), :, rows_used], rs_sem)
         await_bytes(o_send.at[:, pl.ds(0, 7), rows_used], os_sem)
+
+        @pl.when(relay)
+        def _():
+            await_bytes(y_relay.at[:, pl.ds(0, 7), rows_used], pass_sem)
 
 
 def local(bands, fields, cutoff):
@@ -644,6 +680,9 @@
             pltpu.SemaphoreType.REGULAR,
             pltpu.SemaphoreType.REGULAR,
             pltpu.SemaphoreType.REGULAR,
+            vmem((CHUNKS, 8, SLOT, LANES), F32),
+            dma((CHUNKS,)),
+            dma,
         ],
         compiler_params=pltpu.CompilerParams(
             collective_id=0, has_side_effects=True, vmem_limit_bytes=54304 * 1024

time: 44 us -> 42.6 us (0.968)
  Pallas kernels: 42.4 us -> 40.9 us
    pallas_call x1, Pallas kernels: 42.4 us -> 40.9 us  [local(): pl.pallas_call(functools.partial(kernel, bands), out_shape=jax.ShapeDtype...]
where the time goes in v2:
time: 42.6 us; the launch traced here: 42.4 us
  Pallas kernels  40.9 us (96%)
  local copies, waits for them, and re-layouts  1.46 us (3%)
    pallas_call x1, Pallas kernels, local(): pl.pallas_call(functools.partial(kernel, bands), out_shape=jax.ShapeDtype...  40.9 us
    unnamed x3, local copies, waits for them, and re-layouts  1.46 us

profile of v2, /device:TPU:1, one launch (start us, length us, event | category | flops | bytes accessed | tf_op | source)
XLA Modules:
  0.0 42.4 jit_solution(6634388380601729782)
XLA Ops:
  0.0 0.0 copy-start
  0.0 0.7 %copy-done = s32[8]{0:T(128)S(1)} copy-done((s32[8]{0:T(128)S(1)}, s32[8]{0:T(128)}, u32[]{:S(2)}) %copy-start) | copy-done | bytes 56
  0.7 40.9 %shard_map.28 = f32[1080,128]{1,0:T(8,128)S(1)} custom-call(s32[8]{0:T(128)S(1)} %copy-done, f32[1080,128]{1,0:T(8,128)} %bitcast.11), custom_call_target="tpu_custom_call" | custom-call | tf_op jit(solution)/shard_map/pallas_call | solution.py:652
  41.6 0.8 %copy.4 = f32[8,45,384]{2,0,1:T(8,128)} copy(f32[8,45,384]{2,0,1:T(8,128)S(1)} %bitcast.10) | data formatting | bytes 1105920
Async XLA Ops:
  0.0 0.7 %copy-start = (s32[8]{0:T(128)S(1)}, s32[8]{0:T(128)}, u32[]{:S(2)}) copy-start(s32[8]{0:T(128)} %cut_hbm.1) | copy-start | bytes 100

commit v3 on v2

--- a/solution.py
+++ b/solution.py
@@ -447,7 +447,7 @@
     def y_stage(c):
         await_bytes(y_in.at[c, pl.ds(0, 7), rows_used], yr_sem.at[c])
         y_in[c, y, pl.ds(0, HALF)] = y_send[c, row_here, pl.ds(0, HALF)]
-        @pl.loop(0, SLOT, step=8)
+        @pl.loop(0, SLOT, step=8, unroll=True)
         def _(m):
             rows = pl.ds(pl.multiple_of(m, 8), 8)
             pairs = real_dft([y_in[c, i, rows] for i in range(8)])
@@ -496,14 +496,14 @@
 
         @pl.when(x == 0)
         def _():
-            @pl.loop(0, SLOT, step=8)
+            @pl.loop(0, SLOT, step=8, unroll=True)
             def _(m):
                 m = pl.multiple_of(m, 8)
                 write(first_chip_dft([(take(i, 0, m), take(i, 1, m)) for i in range(8)]), m)
 
         @pl.when(x != 0)
         def _():
-            @pl.loop(0, SLOT, step=8)
+            @pl.loop(0, SLOT, step=8, unroll=True)
             def _(m):
                 m = pl.multiple_of(m, 8)
                 write(other_chip_dft([(take(i, 0, m), take(i, 1, m)) for i in range(8)], twist), m)
@@ -530,14 +530,14 @@
 
         @pl.when(x == 0)
         def _():
-            @pl.loop(0, SLOT, step=8)
+            @pl.loop(0, SLOT, step=8, unroll=True)
             def _(m):
                 m = pl.multiple_of(m, 8)
                 write_back(first_chip_idft(pairs_at(m)), m)
 
         @pl.when(x != 0)
         def _():
-            @pl.loop(0, SLOT, step=8)
+            @pl.loop(0, SLOT, step=8, unroll=True)
             def _(m):
                 m = pl.multiple_of(m, 8)
                 write_back(other_chip_idft(pairs_at(m), twist), m)
@@ -554,7 +554,7 @@
             (3, 4),
         )
 
-        @pl.loop(0, SLOT, step=8)
+        @pl.loop(0, SLOT, step=8, unroll=True)
         def _(m):
             rows = pl.ds(pl.multiple_of(m, 8), 8)
             values = real_idft([(r_in[c, g, 0, rows], r_in[c, g, 1, rows]) for g in range(4)])

time: 42.6 us -> 42.4 us (level)
  no operation moved by 1% of the time
where the time goes in v3:
time: 42.4 us; the launch traced here: 42.2 us
  Pallas kernels  40.7 us (96%)
  local copies, waits for them, and re-layouts  1.46 us (3%)
    pallas_call x1, Pallas kernels, local(): pl.pallas_call(functools.partial(kernel, bands), out_shape=jax.ShapeDtype...  40.7 us
    unnamed x3, local copies, waits for them, and re-layouts  1.46 us

profile of v3, /device:TPU:1, one launch (start us, length us, event | category | flops | bytes accessed | tf_op | source)
XLA Modules:
  0.0 42.2 jit_solution(7489982772399016238)
XLA Ops:
  0.0 0.0 copy-start
  0.0 0.7 %copy-done = s32[8]{0:T(128)S(1)} copy-done((s32[8]{0:T(128)S(1)}, s32[8]{0:T(128)}, u32[]{:S(2)}) %copy-start) | copy-done | bytes 56
  0.7 40.7 %shard_map.28 = f32[1080,128]{1,0:T(8,128)S(1)} custom-call(s32[8]{0:T(128)S(1)} %copy-done, f32[1080,128]{1,0:T(8,128)} %bitcast.11), custom_call_target="tpu_custom_call" | custom-call | tf_op jit(solution)/shard_map/pallas_call | solution.py:652
  41.4 0.8 %copy.4 = f32[8,45,384]{2,0,1:T(8,128)} copy(f32[8,45,384]{2,0,1:T(8,128)S(1)} %bitcast.10) | data formatting | bytes 1105920
Async XLA Ops:
  0.0 0.7 %copy-start = (s32[8]{0:T(128)S(1)}, s32[8]{0:T(128)}, u32[]{:S(2)}) copy-start(s32[8]{0:T(128)} %cut_hbm.1) | copy-start | bytes 100
